TPU v7x, 32 devices: a whole 2x2x4 slice. The times are simulated.
32 devices in a mesh: grp: 4 (over y, x), dev: 8 (over z, core).
Axes of the slice: x: 2, y: 2, z: 4, core: 2. Of those that a mesh axis runs over, the one named last changes fastest.
Arguments:
- positions: float32 [3, 32768], P(None, ('grp', 'dev')), may hold values from -6 to 6
- velocities: float32 [3, 32768], P(None, ('grp', 'dev')), may hold values from -6 to 6
- masses: float32 [32768], P(('grp', 'dev')), may hold values from 0.2 to 5
- active_index: int32 [1024], replicated, may hold values from 0 to 32767, as said below
Outputs:
- force: float32 [3, 1024], P(None, ('grp', 'dev'))
- jerk: float32 [3, 1024], P(None, ('grp', 'dev'))
Inputs may be any that keep to these rules, and one draw needn't show every extreme that they name: `active_index`: strictly increasing, distinct indices of stars; at most 64 of them fall in any aligned block of 1024 consecutive stars, and some block holds exactly 64.
All inputs are finite; a program needn't handle non-finite values.
Results may differ from a plain program's by a relative error of at most 0.0003.
Values sent between devices are 32-bit elements; how exact they have to be, the bound alone decides.
A program may use at most 64 MiB of HBM per device.

v0:
```python
import jax
import jax.numpy as jnp
from jax import lax
from jax.sharding import PartitionSpec as P

SOFT = 0.0025


def pair_terms(act_pos, act_vel, pos, vel, mass):
    dx = pos[:, None, :] - act_pos[:, :, None]
    dv = vel[:, None, :] - act_vel[:, :, None]
    r2 = jnp.sum(dx * dx, axis=0) + SOFT
    inv = 1.0 / jnp.sqrt(r2)
    weight = mass[None, :] * inv * inv * inv
    rv = jnp.sum(dx * dv, axis=0)
    acc = jnp.sum(weight[None] * dx, axis=-1)
    jer = jnp.sum(weight[None] * dv - (3.0 * rv * weight / r2)[None] * dx, axis=-1)
    return (acc, jer)


def per_device(positions, velocities, masses, active_index):
    local_count = positions.shape[1]
    groups = lax.axis_size("grp")
    members = lax.axis_size("dev")
    active = active_index.shape[0]
    owner = lax.axis_index("grp") * members + lax.axis_index("dev")
    offset = owner * local_count
    local = active_index - offset
    owned = (local >= 0) & (local < local_count)
    clipped = jnp.clip(local, 0, local_count - 1)
    state = jnp.concatenate(
        [jnp.take(positions, clipped, axis=1), jnp.take(velocities, clipped, axis=1)], axis=0
    )
    state = jnp.where(owned[None, :], state, 0.0)
    state = lax.psum(state, ("grp", "dev"))
    block = min(256, active)
    nblk = active // block
    blocks = state.reshape(6, nblk, block).transpose(1, 0, 2)

    def one_block(item):
        return pair_terms(item[0:3], item[3:6], positions, velocities, masses)

    acc, jer = lax.map(one_block, blocks)
    scale = 1.0 / (local_count * groups * members)
    acc = acc.transpose(1, 0, 2).reshape(3, active) * scale
    jer = jer.transpose(1, 0, 2).reshape(3, active) * scale
    acc, jer = (
        lax.psum_scatter(acc, "grp", scatter_dimension=1, tiled=True),
        lax.psum_scatter(jer, "grp", scatter_dimension=1, tiled=True),
    )
    force, jerk = (
        lax.psum_scatter(acc, "dev", scatter_dimension=1, tiled=True),
        lax.psum_scatter(jer, "dev", scatter_dimension=1, tiled=True),
    )
    return (force, jerk)


def solution(mesh):
    return jax.shard_map(
        per_device,
        mesh=mesh,
        in_specs=(P(None, ("grp", "dev")), P(None, ("grp", "dev")), P(("grp", "dev")), P()),
        out_specs=(P(None, ("grp", "dev")), P(None, ("grp", "dev"))),
        check_vma=False,
    )
```

profile of v0, /device:TPU:0, one launch (start us, length us, event | category | flops | bytes accessed | tf_op | source)
XLA Modules:
  0.0 194.8 jit_solution(9353000239854888546)
XLA Ops:
  7.2 0.0 reduce-scatter.13.cloned.1.call-start
  7.2 0.7 fusion.5
  7.9 0.7 compare_and_fusion.1
  8.6 0.9 copy.18
  9.6 0.9 copy.19
  10.5 2.8 %gather_fusion = f32[1024,3]{1,0:T(8,128)S(1)} fusion(f32[3,1024]{0,1:T(8,128)S(1)} %copy.18, s32[1024]{0:T(1024)S(1)} %fusion.5), kind=kCustom, calls=%fused_computation.clone | custom fusion | bytes 28672 | tf_op jit(solution)/shard_map/jit(_take)/gather | solution.py:32
  13.3 2.8 %gather_fusion.1 = f32[1024,3]{1,0:T(8,128)S(1)} fusion(f32[3,1024]{0,1:T(8,128)S(1)} %copy.19, s32[1024]{0:T(1024)S(1)} %fusion.5), kind=kCustom, calls=%fused_computation.1.clone | custom fusion | bytes 28672 | tf_op jit(solution)/shard_map/jit(_take)/gather | solution.py:32
  16.1 0.2 select_bitcast_fusion.1
  16.4 0.0 copy-start
  16.4 0.0 copy-start.1
  16.4 0.0 copy-start.2
  16.4 0.2 copy.20
  16.6 0.2 copy.21
  16.8 42.1 %psum.7 = f32[4,6,256]{2,1,0:T(8,128)S(1)} all-reduce(f32[4,6,256]{2,1,0:T(8,128)S(1)} %bitcast.37), channel_id=1, replica_groups=mesh['grp'=4,'dev'=8] {'grp','dev'}, use_global_device_ids=true, to_apply=%region_0.2 | all-reduce | flops 6144 | bytes 49152 | tf_op jit(solution)/shard_map/psum | solution.py:35
  58.9 0.0 copy-done
  58.9 0.0 copy-done.1
  59.0 0.0 copy-done.2
  59.0 10.1 %while.12 = (s32[]{:T(128)}, f32[4,3,256]{2,1,0:T(4,128)S(1)}, f32[4,3,256]{2,1,0:T(4,128)S(1)}, f32[3,1024]{1,0:T(4,128)S(1)}, f32[4,6,256]{2,1,0:T(8,128)S(1)}...) while((s32[]{:T(128)}, f32[4,3,256]{2,1,0:T(4,128)S(1)}, ...), condition=%wide.region_6.8_spmd, body=%wide.region_1.7_spmd.sunk | while | flops 12319235 | bytes 8489085 | solution.py:43
  59.0 0.7 fusion.8
  59.7 0.3 multiply_multiply_fusion.2
  60.0 1.5 fusion.9
  61.5 0.7 fusion.8
  62.2 0.3 multiply_multiply_fusion.2
  62.5 1.5 fusion.9
  64.0 0.7 fusion.8
  64.7 0.3 multiply_multiply_fusion.2
  65.1 1.5 fusion.9
  66.6 0.7 fusion.8
  67.3 0.3 multiply_multiply_fusion.2
  67.6 1.5 fusion.9
  69.1 1.0 copy.25
  70.1 0.0 reduce-scatter.13.cloned.1.call-update
  70.1 0.0 reduce-scatter.17.cloned.1.call-start
  70.2 1.0 copy.29
  71.2 0.0 reduce-scatter.17.cloned.1.call-update
  71.3 0.0 reduce-scatter.15.cloned.1.call-start
  71.3 23.9 %reduce-scatter.13.cloned.1.call-done = f32[256,3]{1,0:T(8,128)} async-done(((f32[1024,3]{1,0:T(8,128)}), f32[256,3]{1,0:T(8,128)}) %reduce-scatter.13.cloned.1.call-update) | async-done | bytes 3088
  95.2 0.0 reduce-scatter.15.cloned.1.call-update
  95.3 0.0 reduce-scatter.19.cloned.1.call-start
  95.3 27.9 %reduce-scatter.17.cloned.1.call-done = f32[256,3]{1,0:T(8,128)} async-done(((f32[1024,3]{1,0:T(8,128)}), f32[256,3]{1,0:T(8,128)}) %reduce-scatter.17.cloned.1.call-update) | async-done | bytes 3088
  123.2 0.0 reduce-scatter.19.cloned.1.call-update
  123.2 32.8 %reduce-scatter.15.cloned.1.call-done = f32[32,3]{1,0:T(8,128)} async-done(((f32[256,3]{1,0:T(8,128)}), f32[32,3]{1,0:T(8,128)}) %reduce-scatter.15.cloned.1.call-update) | async-done | bytes 400
  156.1 1.4 copy.28
  157.4 29.5 %reduce-scatter.19.cloned.1.call-done = f32[32,3]{1,0:T(8,128)} async-done(((f32[256,3]{1,0:T(8,128)}), f32[32,3]{1,0:T(8,128)}) %reduce-scatter.19.cloned.1.call-update) | async-done | bytes 400
  186.9 1.4 copy.32
  (12 shorter events, 0.1 us)
Async XLA Ops:
  7.2 88.1 %reduce-scatter.13.cloned.1.call-start = ((), (), s32[]{:S(2)}) async-start(), calls=%async_computation.4 | async-start | bytes 655360
  16.4 42.6 %copy-start = (f32[3,1024]{1,0:T(4,128)S(1)}, f32[3,1024]{1,0:T(4,128)}, u32[]{:S(2)}) copy-start(f32[3,1024]{1,0:T(4,128)} %param.8) | copy-start | bytes 36868
  16.4 42.6 %copy-start.1 = (f32[3,1024]{1,0:T(4,128)S(1)}, f32[3,1024]{1,0:T(4,128)}, u32[]{:S(2)}) copy-start(f32[3,1024]{1,0:T(4,128)} %param.9) | copy-start | bytes 36868
  16.4 42.6 %copy-start.2 = (f32[1024]{0:T(1024)S(1)}, f32[1024]{0:T(1024)}, u32[]{:S(2)}) copy-start(f32[1024]{0:T(1024)} %param.10) | copy-start | bytes 12292
  70.1 53.1 %reduce-scatter.17.cloned.1.call-start = ((), (), s32[]{:S(2)}) async-start(), calls=%async_computation.6 | async-start | bytes 655360
  71.3 84.8 %reduce-scatter.15.cloned.1.call-start = ((), (), s32[]{:S(2)}) async-start(), calls=%async_computation.5 | async-start | bytes 147456
  95.3 91.7 %reduce-scatter.19.cloned.1.call-start = ((), (), s32[]{:S(2)}) async-start(), calls=%async_computation.7 | async-start | bytes 147456
Sparse Core Ops, SparseCore 0:
  70.3 24.9 reduce-scatter.12
  98.0 25.1 reduce-scatter.16
  125.5 30.5 reduce-scatter.14
  158.2 28.7 reduce-scatter.18
where the time goes:
time: 196 us; the launch traced here: 195 us
  waiting for transfers between devices  114 us (58%)
  blocking collectives  42.1 us (21%)
  between operations  13.9 us (7%)
  local copies, waits for them, and re-layouts  12.8 us (7%)
  other arithmetic  11.5 us (6%)
    unnamed x8, waiting for transfers between devices  114 us
    psum x1, blocking collectives, per_device(): state = lax.psum(state, ('grp', 'dev'))  42.1 us
    unnamed x12, local copies, waits for them, and re-layouts  6.69 us
    reduce_sum x4, other arithmetic, pair_terms(): jnp.sum(weight[None] * dv - (3.0 * rv * weight / r2)[None] * dx, axis=-1)  5.84 us
  transfers between devices with their start and end apart: 4, of which 4 were waited for; matrix products, arithmetic and copies ran while one was open for 1% of the time, Pallas kernels for 0%

commit v1 on v0

--- a/solution.py
+++ b/solution.py
@@ -1,9 +1,16 @@
+import functools
+
 import jax
 import jax.numpy as jnp
 from jax import lax
+from jax.experimental import pallas as pl
+from jax.experimental.pallas import tpu as pltpu
 from jax.sharding import PartitionSpec as P
 
 SOFT = 0.0025
+SUB, LANE = 8, 128
+HALF = LANE // 2
+UNROLL = 8
 
 
 def pair_terms(act_pos, act_vel, pos, vel, mass):
@@ -42,22 +49,190 @@
 
     acc, jer = lax.map(one_block, blocks)
     scale = 1.0 / (local_count * groups * members)
-    acc = acc.transpose(1, 0, 2).reshape(3, active) * scale
-    jer = jer.transpose(1, 0, 2).reshape(3, active) * scale
-    acc, jer = (
-        lax.psum_scatter(acc, "grp", scatter_dimension=1, tiled=True),
-        lax.psum_scatter(jer, "grp", scatter_dimension=1, tiled=True),
+    both = jnp.concatenate(
+        [acc.transpose(1, 0, 2).reshape(3, active), jer.transpose(1, 0, 2).reshape(3, active)], axis=0
     )
-    force, jerk = (
-        lax.psum_scatter(acc, "dev", scatter_dimension=1, tiled=True),
-        lax.psum_scatter(jer, "dev", scatter_dimension=1, tiled=True),
-    )
-    return (force, jerk)
+    both = lax.psum_scatter(both * scale, ("grp", "dev"), scatter_dimension=1, tiled=True)
+    return (both[0:3], both[3:6])
+
+
+def kernel(groups, members, idx_ref, pos_ref, vel_ref, pos_s, vel_s, mass_s, force_ref, jerk_ref,
+           mine, got, part, parts, send_a, recv_a, send_b, recv_b):
+    ndev = groups * members
+    count = pos_ref.shape[1]
+    per = force_ref.shape[1]
+    ngrp = LANE // per
+    me = lax.axis_index("grp") * members + lax.axis_index("dev")
+
+    def place(k):
+        other = lax.rem(me + k, ndev)
+        return other, (lax.div(other, members), lax.rem(other, members))
+
+    barrier = pltpu.get_barrier_semaphore()
+
+    def greet(k, c):
+        pl.semaphore_signal(barrier, inc=1, device_id=place(k)[1], device_id_type=pl.DeviceIdType.MESH)
+        return c
+
+    lax.fori_loop(1, ndev, greet, 0)
+
+    idx = idx_ref[...]
+    local = idx - me * count
+    owned = (local >= 0) & (local < count)
+    slot = jnp.sum(jnp.where(owned, local + 1, 0), axis=0, keepdims=True)
+    slot = slot + pltpu.roll(slot, HALF, 1)
+    pick = (lax.broadcasted_iota(jnp.int32, (count, LANE), 0) + 1 == slot).astype(jnp.float32)
+    up = jnp.dot(pos_ref[...], pick, precision=lax.Precision.HIGHEST, preferred_element_type=jnp.float32)
+    uv = jnp.dot(vel_ref[...], pick, precision=lax.Precision.HIGHEST, preferred_element_type=jnp.float32)
+    lane3 = lax.broadcasted_iota(jnp.int32, (3, LANE), 1)
+    own = jnp.where(lane3 < HALF, up, uv)
+    mine[...] = own
+    got[me] = own
+
+    pl.semaphore_wait(barrier, ndev - 1)
+
+    def gather_copy(k, sender):
+        other, where = place(k)
+        return pltpu.make_async_remote_copy(
+            src_ref=mine, dst_ref=got.at[sender], send_sem=send_a.at[other], recv_sem=recv_a.at[sender],
+            device_id=where, device_id_type=pl.DeviceIdType.MESH)
+
+    def start_a(k, c):
+        gather_copy(k, me).start()
+        return c
+
+    def wait_a(k, c):
+        gather_copy(k, place(k)[0]).wait_recv()
+        return c
+
+    def sent_a(k, c):
+        gather_copy(k, me).wait_send()
+        return c
+
+    lax.fori_loop(1, ndev, start_a, 0)
+    lax.fori_loop(1, ndev, wait_a, 0)
+
+    same = [jnp.zeros((SUB, LANE), jnp.float32)] * 3
+    swap = [jnp.zeros((SUB, LANE), jnp.float32)] * 3
+    for d in range(ndev):
+        rows = got[d]
+        turned = pltpu.roll(rows, HALF, 1)
+        from_d = idx >= d * count
+        for i in range(3):
+            same[i] = jnp.where(from_d, jnp.broadcast_to(rows[i:i + 1], (SUB, LANE)), same[i])
+            swap[i] = jnp.where(from_d, jnp.broadcast_to(turned[i:i + 1], (SUB, LANE)), swap[i])
+    lane = lax.broadcasted_iota(jnp.int32, (SUB, LANE), 1)
+    ap = [jnp.where(lane < HALF, same[i], swap[i]) for i in range(3)]
+    av = [jnp.where(lane < HALF, swap[i], same[i]) for i in range(3)]
+
+    def step(b, sums):
+        sums = list(sums)
+        for u in range(UNROLL):
+            j = b * UNROLL + u
+            dx = [pos_s[i, j] - ap[i] for i in range(3)]
+            dv = [vel_s[i, j] - av[i] for i in range(3)]
+            r2 = dx[0] * dx[0] + dx[1] * dx[1] + (dx[2] * dx[2] + SOFT)
+            inv = lax.rsqrt(r2)
+            inv2 = inv * inv
+            weight = (mass_s[j] * inv) * inv2
+            rv = dx[0] * dv[0] + dx[1] * dv[1] + dx[2] * dv[2]
+            bend = (rv * inv2) * weight
+            for i in range(3):
+                sums[i] = sums[i] + weight * dx[i]
+                sums[3 + i] = sums[3 + i] + weight * dv[i]
+                sums[6 + i] = sums[6 + i] + bend * dx[i]
+        return tuple(sums)
+
+    zero = jnp.zeros((SUB, LANE), jnp.float32)
+    sums = lax.fori_loop(0, count // UNROLL, step, (zero,) * 9)
+    scale = 1.0 / (count * ndev)
+    outs = [sums[i] * scale for i in range(3)]
+    outs += [(sums[3 + i] - 3.0 * sums[6 + i]) * scale for i in range(3)]
+
+    kind = lax.div(lane, per)
+    nrow = part.shape[2]
+    for g in range(ngrp):
+        for r in range(nrow):
+            packed = zero
+            for f in range(min(ngrp, 6 - ngrp * r)):
+                value = outs[ngrp * r + f]
+                turn = per * ((f - g) % ngrp)
+                if turn:
+                    value = pltpu.roll(value, turn, 1)
+                packed = jnp.where(kind == f, value, packed)
+            part[:, g, r, :] = packed
+
+    def scatter_copy(k, sender):
+        other, where = place(k)
+        return pltpu.make_async_remote_copy(
+            src_ref=part.at[lax.div(other, ngrp), lax.rem(other, ngrp)], dst_ref=parts.at[sender],
+            send_sem=send_b.at[other], recv_sem=recv_b.at[sender],
+            device_id=where, device_id_type=pl.DeviceIdType.MESH)
+
+    def start_b(k, c):
+        scatter_copy(k, me).start()
+        return c
+
+    def wait_b(k, c):
+        scatter_copy(k, place(k)[0]).wait_recv()
+        return c
+
+    def sent_b(k, c):
+        scatter_copy(k, me).wait_send()
+        return c
+
+    lax.fori_loop(1, ndev, start_b, 0)
+    parts[me] = part[lax.div(me, ngrp), lax.rem(me, ngrp)]
+    lax.fori_loop(1, ndev, sent_a, 0)
+    lax.fori_loop(1, ndev, wait_b, 0)
+    total = jnp.sum(parts[...], axis=0)
+    for f in range(6):
+        r, c = f // ngrp, (f % ngrp) * per
+        out_ref = force_ref if f < 3 else jerk_ref
+        out_ref[f % 3:f % 3 + 1, :] = total[r:r + 1, c:c + per]
+    lax.fori_loop(1, ndev, sent_b, 0)
+
+
+def fused(groups, members, positions, velocities, masses, active_index):
+    ndev = groups * members
+    per = active_index.shape[0] // ndev
+    ngrp = LANE // per
+    nrow = -(-6 // ngrp)
+    vmem = pl.BlockSpec(memory_space=pltpu.VMEM)
+    smem = pl.BlockSpec(memory_space=pltpu.SMEM)
+    out = jax.ShapeDtypeStruct((3, per), jnp.float32)
+    sems = pltpu.SemaphoreType.DMA((ndev,))
+    return pl.pallas_call(
+        functools.partial(kernel, groups, members),
+        out_shape=(out, out),
+        in_specs=[vmem, vmem, vmem, smem, smem, smem],
+        out_specs=(vmem, vmem),
+        scratch_shapes=[
+            pltpu.VMEM((3, LANE), jnp.float32),
+            pltpu.VMEM((ndev, 3, LANE), jnp.float32),
+            pltpu.VMEM((ndev // ngrp, ngrp, nrow, LANE), jnp.float32),
+            pltpu.VMEM((ndev, nrow, LANE), jnp.float32),
+            sems, sems, sems, sems,
+        ],
+        compiler_params=pltpu.CompilerParams(collective_id=0, has_side_effects=True),
+        name="hermite",
+    )(active_index.reshape(SUB, LANE), positions, velocities, positions, velocities, masses)
 
 
 def solution(mesh):
+    groups, members = mesh.shape["grp"], mesh.shape["dev"]
+    ndev = groups * members
+
+    def body(positions, velocities, masses, active_index):
+        active, count = active_index.shape[0], positions.shape[1]
+        per = active // ndev
+        fits = active == SUB * LANE and LANE % per == 0 and ndev == SUB * (LANE // per)
+        if fits and 2 * per == HALF and count % UNROLL == 0:
+            return fused(groups, members, positions, velocities, masses, active_index)
+        return per_device(positions, velocities, masses, active_index)
+
     return jax.shard_map(
-        per_device,
+        body,
         mesh=mesh,
         in_specs=(P(None, ("grp", "dev")), P(None, ("grp", "dev")), P(("grp", "dev")), P()),
         out_specs=(P(None, ("grp", "dev")), P(None, ("grp", "dev"))),

time: 196 us -> 30.8 us (0.16)
  waiting for transfers between devices: 114 us -> 0 us
  blocking collectives: 42.1 us -> 0 us
  Pallas kernels: 0 us -> 28 us
  between operations: 13.9 us -> 0.65 us
  other arithmetic: 11.5 us -> 0 us
  local copies, waits for them, and re-layouts: 12.8 us -> 1.89 us
    unnamed x8 -> x0, waiting for transfers between devices: 114 us -> none
    psum x1 -> x0, blocking collectives: 42.1 us -> none  [per_device(): state = lax.psum(state, ('grp', 'dev'))]
    pallas_call x0 -> x1, Pallas kernels: none -> 28 us  [fused(): pl.pallas_call(functools.partial(kernel, groups, members), out_shape=(out...]
    reduce_sum x8 -> x0, other arithmetic: 8.53 us -> none  [the longest x4 5.84 us: pair_terms(): jnp.sum(weight[None] * dv - (3.0 * rv * weight / r2)[None] * dx, axis=-1)]
    gather x2 -> x0, local copies, waits for them, and re-layouts: 5.63 us -> none  [the longest x1 2.81 us: per_device(): jnp.take(positions, clipped, axis=1)]
    unnamed x12 -> x6, local copies, waits for them, and re-layouts: 6.69 us -> 1.89 us
  transfers between devices with their start and end apart: 4 -> 0, of which waited for: 4 -> 0; matrix products, arithmetic and copies ran while one was open for 1% -> 0% of each run, Pallas kernels for 0% -> 0%
where the time goes in v1:
time: 30.8 us; the launch traced here: 30.5 us
  Pallas kernels  28 us (91%)
  local copies, waits for them, and re-layouts  1.89 us (6%)
  between operations  0.65 us (2%)
    pallas_call x1, Pallas kernels, fused(): pl.pallas_call(functools.partial(kernel, groups, members), out_shape=(out...  28 us
    unnamed x6, local copies, waits for them, and re-layouts  1.89 us

profile of v1, /device:TPU:0, one launch (start us, length us, event | category | flops | bytes accessed | tf_op | source)
XLA Modules:
  0.0 30.5 jit_solution(5106217600286202248)
XLA Ops:
  0.6 28.0 %hermite.1 = (f32[3,32]{1,0:T(4,128)}, f32[3,32]{1,0:T(4,128)}) custom-call(s32[8,128]{1,0:T(8,128)} %bitcast.1, f32[3,1024]{1,0:T(4,128)} %pos_s.1, f32[3,1024]{1,0:T(4,128)} %vel_s.1, f32[3,1024]{1,0:T(4,128)} %pos_s.1, f32[3,1024]{1,0:T(4,128)} %vel_s.1, f32[1024]{0:T(1024)} %mass_s.1), custom_call_target="tpu_custom_call" | custom-call | tf_op jit(solution)/shard_map/hermite/pallas_call | solution.py:205
  28.6 0.0 copy-start.1
  28.6 0.7 %copy-done.1 = f32[3,32]{1,0:T(4,128)S(1)} copy-done((f32[3,32]{1,0:T(4,128)S(1)}, f32[3,32]{1,0:T(4,128)}, u32[]{:S(2)}) %copy-start.1) | copy-done | bytes 408
  29.3 0.0 copy-start
  29.3 0.6 %copy.8 = f32[3,32]{1,0:T(4,128)} copy(f32[3,32]{1,0:T(4,128)S(1)} %copy-done.1) | data formatting | bytes 768
  29.9 0.1 copy-done
  30.0 0.6 %copy.9 = f32[3,32]{1,0:T(4,128)} copy(f32[3,32]{1,0:T(4,128)S(1)} %copy-done) | data formatting | bytes 768
Async XLA Ops:
  28.6 0.7 %copy-start.1 = (f32[3,32]{1,0:T(4,128)S(1)}, f32[3,32]{1,0:T(4,128)}, u32[]{:S(2)}) copy-start(f32[3,32]{1,0:T(4,128)} %get-tuple-element.4) | copy-start | bytes 1156
  29.3 0.7 %copy-start = (f32[3,32]{1,0:T(4,128)S(1)}, f32[3,32]{1,0:T(4,128)}, u32[]{:S(2)}) copy-start(f32[3,32]{1,0:T(4,128)} %get-tuple-element.5) | copy-start | bytes 1156

commit v2 on v1

--- a/solution.py
+++ b/solution.py
@@ -56,25 +56,35 @@
     return (both[0:3], both[3:6])
 
 
-def kernel(groups, members, idx_ref, pos_ref, vel_ref, pos_s, vel_s, mass_s, force_ref, jerk_ref,
-           mine, got, part, parts, send_a, recv_a, send_b, recv_b):
+def kernel(groups, members, idx_h, pos_h, vel_h, mass_h, both_ref,
+           idx_ref, stars, mass_ref, wide, got, part, parts,
+           load_sem, send_g, recv_g, send_d, recv_d, send_b, recv_b):
     ndev = groups * members
-    count = pos_ref.shape[1]
-    per = force_ref.shape[1]
+    count = pos_h.shape[1]
+    chunks = count // LANE
+    per = both_ref.shape[2]
     ngrp = LANE // per
-    me = lax.axis_index("grp") * members + lax.axis_index("dev")
-
-    def place(k):
-        other = lax.rem(me + k, ndev)
-        return other, (lax.div(other, members), lax.rem(other, members))
+    my_g, my_d = lax.axis_index("grp"), lax.axis_index("dev")
+    me = my_g * members + my_d
 
     barrier = pltpu.get_barrier_semaphore()
-
-    def greet(k, c):
-        pl.semaphore_signal(barrier, inc=1, device_id=place(k)[1], device_id_type=pl.DeviceIdType.MESH)
-        return c
-
-    lax.fori_loop(1, ndev, greet, 0)
+    for k in range(1, groups):
+        pl.semaphore_signal(barrier, inc=1, device_id=(lax.rem(my_g + k, groups), my_d),
+                            device_id_type=pl.DeviceIdType.MESH)
+    for k in range(1, members):
+        pl.semaphore_signal(barrier, inc=1, device_id=(my_g, lax.rem(my_d + k, members)),
+                            device_id_type=pl.DeviceIdType.MESH)
+
+    loads = [
+        pltpu.make_async_copy(idx_h, idx_ref, load_sem.at[0]),
+        pltpu.make_async_copy(pos_h, stars.at[0], load_sem.at[1]),
+        pltpu.make_async_copy(vel_h, stars.at[1], load_sem.at[2]),
+        pltpu.make_async_copy(mass_h, mass_ref, load_sem.at[3]),
+    ]
+    for copy in loads:
+        copy.start()
+    for copy in loads:
+        copy.wait()
 
     idx = idx_ref[...]
     local = idx - me * count
@@ -82,40 +92,53 @@
     slot = jnp.sum(jnp.where(owned, local + 1, 0), axis=0, keepdims=True)
     slot = slot + pltpu.roll(slot, HALF, 1)
     pick = (lax.broadcasted_iota(jnp.int32, (count, LANE), 0) + 1 == slot).astype(jnp.float32)
-    up = jnp.dot(pos_ref[...], pick, precision=lax.Precision.HIGHEST, preferred_element_type=jnp.float32)
-    uv = jnp.dot(vel_ref[...], pick, precision=lax.Precision.HIGHEST, preferred_element_type=jnp.float32)
+    state = jnp.concatenate([stars[0], stars[1]], axis=0)
+    picked = jnp.dot(state, pick, precision=lax.Precision.HIGHEST, preferred_element_type=jnp.float32)
     lane3 = lax.broadcasted_iota(jnp.int32, (3, LANE), 1)
-    own = jnp.where(lane3 < HALF, up, uv)
-    mine[...] = own
-    got[me] = own
-
-    pl.semaphore_wait(barrier, ndev - 1)
-
-    def gather_copy(k, sender):
-        other, where = place(k)
+    got[my_d, my_g] = jnp.where(lane3 < HALF, picked[0:3], picked[3:6])
+
+    pl.semaphore_wait(barrier, groups + members - 2)
+
+    def group_copy(k, sender):
+        g = lax.rem(my_g + k, groups)
         return pltpu.make_async_remote_copy(
-            src_ref=mine, dst_ref=got.at[sender], send_sem=send_a.at[other], recv_sem=recv_a.at[sender],
-            device_id=where, device_id_type=pl.DeviceIdType.MESH)
-
-    def start_a(k, c):
-        gather_copy(k, me).start()
-        return c
-
-    def wait_a(k, c):
-        gather_copy(k, place(k)[0]).wait_recv()
-        return c
-
-    def sent_a(k, c):
-        gather_copy(k, me).wait_send()
-        return c
-
-    lax.fori_loop(1, ndev, start_a, 0)
-    lax.fori_loop(1, ndev, wait_a, 0)
+            src_ref=got.at[my_d, my_g], dst_ref=got.at[my_d, sender],
+            send_sem=send_g.at[g], recv_sem=recv_g.at[sender],
+            device_id=(g, my_d), device_id_type=pl.DeviceIdType.MESH)
+
+    def member_copy(k, sender):
+        d = lax.rem(my_d + k, members)
+        return pltpu.make_async_remote_copy(
+            src_ref=got.at[my_d], dst_ref=got.at[sender],
+            send_sem=send_d.at[d], recv_sem=recv_d.at[sender],
+            device_id=(my_g, d), device_id_type=pl.DeviceIdType.MESH)
+
+    for k in range(1, groups):
+        group_copy(k, my_g).start()
+
+    def spread(c, carry):
+        at = pl.ds(pl.multiple_of(c * LANE, LANE), LANE)
+        rows = jnp.concatenate(
+            [stars[0, :, at], stars[1, :, at], mass_ref[pl.ds(c, 1), :], mass_ref[pl.ds(c, 1), :]], axis=0)
+        cols = jnp.transpose(rows)
+        for f in range(7):
+            wide[f, at, :] = jnp.broadcast_to(cols[:, f:f + 1], (LANE, LANE))
+        return carry
+
+    first = chunks // 4
+    lax.fori_loop(0, first, spread, 0)
+    for k in range(1, groups):
+        group_copy(k, lax.rem(my_g + k, groups)).wait_recv()
+    for k in range(1, members):
+        member_copy(k, my_d).start()
+    lax.fori_loop(first, chunks, spread, 0)
+    for k in range(1, members):
+        member_copy(k, lax.rem(my_d + k, members)).wait_recv()
 
     same = [jnp.zeros((SUB, LANE), jnp.float32)] * 3
     swap = [jnp.zeros((SUB, LANE), jnp.float32)] * 3
     for d in range(ndev):
-        rows = got[d]
+        rows = got[d % members, d // members]
         turned = pltpu.roll(rows, HALF, 1)
         from_d = idx >= d * count
         for i in range(3):
@@ -127,14 +150,15 @@
 
     def step(b, sums):
         sums = list(sums)
+        base = pl.multiple_of(b * UNROLL, UNROLL)
         for u in range(UNROLL):
-            j = b * UNROLL + u
-            dx = [pos_s[i, j] - ap[i] for i in range(3)]
-            dv = [vel_s[i, j] - av[i] for i in range(3)]
+            star = [jnp.broadcast_to(wide[f, pl.ds(base + u, 1), :], (SUB, LANE)) for f in range(7)]
+            dx = [star[i] - ap[i] for i in range(3)]
+            dv = [star[3 + i] - av[i] for i in range(3)]
             r2 = dx[0] * dx[0] + dx[1] * dx[1] + (dx[2] * dx[2] + SOFT)
             inv = lax.rsqrt(r2)
             inv2 = inv * inv
-            weight = (mass_s[j] * inv) * inv2
+            weight = (star[6] * inv) * inv2
             rv = dx[0] * dv[0] + dx[1] * dv[1] + dx[2] * dv[2]
             bend = (rv * inv2) * weight
             for i in range(3):
@@ -163,18 +187,19 @@
             part[:, g, r, :] = packed
 
     def scatter_copy(k, sender):
-        other, where = place(k)
+        other = lax.rem(me + k, ndev)
         return pltpu.make_async_remote_copy(
             src_ref=part.at[lax.div(other, ngrp), lax.rem(other, ngrp)], dst_ref=parts.at[sender],
             send_sem=send_b.at[other], recv_sem=recv_b.at[sender],
-            device_id=where, device_id_type=pl.DeviceIdType.MESH)
+            device_id=(lax.div(other, members), lax.rem(other, members)),
+            device_id_type=pl.DeviceIdType.MESH)
 
     def start_b(k, c):
         scatter_copy(k, me).start()
         return c
 
     def wait_b(k, c):
-        scatter_copy(k, place(k)[0]).wait_recv()
+        scatter_copy(k, lax.rem(me + k, ndev)).wait_recv()
         return c
 
     def sent_b(k, c):
@@ -183,40 +208,45 @@
 
     lax.fori_loop(1, ndev, start_b, 0)
     parts[me] = part[lax.div(me, ngrp), lax.rem(me, ngrp)]
-    lax.fori_loop(1, ndev, sent_a, 0)
+    for k in range(1, groups):
+        group_copy(k, my_g).wait_send()
+    for k in range(1, members):
+        member_copy(k, my_d).wait_send()
+    lax.fori_loop(1, ndev, sent_b, 0)
     lax.fori_loop(1, ndev, wait_b, 0)
     total = jnp.sum(parts[...], axis=0)
     for f in range(6):
         r, c = f // ngrp, (f % ngrp) * per
-        out_ref = force_ref if f < 3 else jerk_ref
-        out_ref[f % 3:f % 3 + 1, :] = total[r:r + 1, c:c + per]
-    lax.fori_loop(1, ndev, sent_b, 0)
+        both_ref[f // 3, f % 3:f % 3 + 1, :] = total[r:r + 1, c:c + per]
 
 
 def fused(groups, members, positions, velocities, masses, active_index):
     ndev = groups * members
+    count = positions.shape[1]
     per = active_index.shape[0] // ndev
     ngrp = LANE // per
     nrow = -(-6 // ngrp)
-    vmem = pl.BlockSpec(memory_space=pltpu.VMEM)
-    smem = pl.BlockSpec(memory_space=pltpu.SMEM)
-    out = jax.ShapeDtypeStruct((3, per), jnp.float32)
-    sems = pltpu.SemaphoreType.DMA((ndev,))
-    return pl.pallas_call(
+    sems = pltpu.SemaphoreType.DMA
+    both = pl.pallas_call(
         functools.partial(kernel, groups, members),
-        out_shape=(out, out),
-        in_specs=[vmem, vmem, vmem, smem, smem, smem],
-        out_specs=(vmem, vmem),
+        out_shape=jax.ShapeDtypeStruct((2, 3, per), jnp.float32),
+        in_specs=[pl.BlockSpec(memory_space=pl.ANY)] * 4,
+        out_specs=pl.BlockSpec(memory_space=pltpu.VMEM),
         scratch_shapes=[
-            pltpu.VMEM((3, LANE), jnp.float32),
-            pltpu.VMEM((ndev, 3, LANE), jnp.float32),
+            pltpu.VMEM((SUB, LANE), jnp.int32),
+            pltpu.VMEM((2, 3, count), jnp.float32),
+            pltpu.VMEM((count // LANE, LANE), jnp.float32),
+            pltpu.VMEM((7, count, LANE), jnp.float32),
+            pltpu.VMEM((members, groups, 3, LANE), jnp.float32),
             pltpu.VMEM((ndev // ngrp, ngrp, nrow, LANE), jnp.float32),
             pltpu.VMEM((ndev, nrow, LANE), jnp.float32),
-            sems, sems, sems, sems,
+            sems((4,)), sems((groups,)), sems((groups,)), sems((members,)), sems((members,)),
+            sems((ndev,)), sems((ndev,)),
         ],
         compiler_params=pltpu.CompilerParams(collective_id=0, has_side_effects=True),
         name="hermite",
-    )(active_index.reshape(SUB, LANE), positions, velocities, positions, velocities, masses)
+    )(active_index.reshape(SUB, LANE), positions, velocities, masses.reshape(count // LANE, LANE))
+    return both[0], both[1]
 
 
 def solution(mesh):
@@ -227,7 +257,7 @@
         active, count = active_index.shape[0], positions.shape[1]
         per = active // ndev
         fits = active == SUB * LANE and LANE % per == 0 and ndev == SUB * (LANE // per)
-        if fits and 2 * per == HALF and count % UNROLL == 0:
+        if fits and 2 * per == HALF and count % (SUB * LANE) == 0:
             return fused(groups, members, positions, velocities, masses, active_index)
         return per_device(positions, velocities, masses, active_index)
 

time: 30.8 us -> 27.3 us (0.89)
  Pallas kernels: 28 us -> 25.2 us
  local copies, waits for them, and re-layouts: 1.89 us -> 1.26 us
    pallas_call x1, Pallas kernels: 28 us -> 25.2 us  [fused(): pl.pallas_call(functools.partial(kernel, groups, members), out_shape=jax....]
    unnamed x6 -> x0, local copies, waits for them, and re-layouts: 1.89 us -> none
    squeeze x0 -> x1, local copies, waits for them, and re-layouts: none -> 1.26 us  [fused(): return (both[0], both[1])]
where the time goes in v2:
time: 27.3 us; the launch traced here: 27.1 us
  Pallas kernels  25.2 us (92%)
  local copies, waits for them, and re-layouts  1.26 us (5%)
  between operations  0.64 us (2%)
    pallas_call x1, Pallas kernels, fused(): pl.pallas_call(functools.partial(kernel, groups, members), out_shape=jax....  25.2 us
    squeeze x1, local copies, waits for them, and re-layouts, fused(): return (both[0], both[1])  1.26 us

profile of v2, /device:TPU:0, one launch (start us, length us, event | category | flops | bytes accessed | tf_op | source)
XLA Modules:
  0.0 27.1 jit_solution(8589761710444779702)
XLA Ops:
  0.6 25.2 %hermite.1 = f32[2,3,32]{2,1,0:T(4,128)} custom-call(s32[8,128]{1,0:T(8,128)} %bitcast.6, f32[3,1024]{1,0:T(4,128)} %pos_h.1, f32[3,1024]{1,0:T(4,128)} %vel_h.1, f32[8,128]{1,0:T(8,128)} %bitcast.7), custom_call_target="tpu_custom_call" | custom-call | tf_op jit(solution)/shard_map/hermite/pallas_call | solution.py:230
  25.8 1.3 %slice_bitcast_fusion = (f32[3,32]{1,0:T(4,128)}, f32[3,32]{1,0:T(4,128)}) fusion(f32[2,3,32]{2,1,0:T(4,128)} %hermite.1), kind=kLoop, calls=%fused_computation | loop fusion | bytes 1536 | tf_op jit(solution)/shard_map/squeeze | solution.py:249

commit v3 on v2

--- a/solution.py
+++ b/solution.py
@@ -10,7 +10,7 @@
 SOFT = 0.0025
 SUB, LANE = 8, 128
 HALF = LANE // 2
-UNROLL = 8
+UNROLL = 16
 
 
 def pair_terms(act_pos, act_vel, pos, vel, mass):
@@ -83,8 +83,7 @@
     ]
     for copy in loads:
         copy.start()
-    for copy in loads:
-        copy.wait()
+    loads[0].wait()
 
     idx = idx_ref[...]
     local = idx - me * count
@@ -92,29 +91,38 @@
     slot = jnp.sum(jnp.where(owned, local + 1, 0), axis=0, keepdims=True)
     slot = slot + pltpu.roll(slot, HALF, 1)
     pick = (lax.broadcasted_iota(jnp.int32, (count, LANE), 0) + 1 == slot).astype(jnp.float32)
+    pick = pick.astype(jnp.bfloat16)
+    for copy in loads[1:]:
+        copy.wait()
     state = jnp.concatenate([stars[0], stars[1]], axis=0)
-    picked = jnp.dot(state, pick, precision=lax.Precision.HIGHEST, preferred_element_type=jnp.float32)
+    high = state.astype(jnp.bfloat16).astype(jnp.float32)
+    rest = state - high
+    middle = rest.astype(jnp.bfloat16).astype(jnp.float32)
+    fill = jnp.zeros((2, count), jnp.float32)
+    pieces = jnp.concatenate([high, fill, middle, fill, rest - middle, fill], axis=0).astype(jnp.bfloat16)
+    picked = jnp.dot(pieces, pick, preferred_element_type=jnp.float32)
+    picked = (picked[0:8] + picked[8:16]) + picked[16:24]
     lane3 = lax.broadcasted_iota(jnp.int32, (3, LANE), 1)
-    got[my_d, my_g] = jnp.where(lane3 < HALF, picked[0:3], picked[3:6])
+    got[my_g, my_d] = jnp.where(lane3 < HALF, picked[0:3], picked[3:6])
 
     pl.semaphore_wait(barrier, groups + members - 2)
 
     def group_copy(k, sender):
         g = lax.rem(my_g + k, groups)
         return pltpu.make_async_remote_copy(
-            src_ref=got.at[my_d, my_g], dst_ref=got.at[my_d, sender],
+            src_ref=got.at[my_g], dst_ref=got.at[sender],
             send_sem=send_g.at[g], recv_sem=recv_g.at[sender],
             device_id=(g, my_d), device_id_type=pl.DeviceIdType.MESH)
 
     def member_copy(k, sender):
         d = lax.rem(my_d + k, members)
         return pltpu.make_async_remote_copy(
-            src_ref=got.at[my_d], dst_ref=got.at[sender],
+            src_ref=got.at[my_g, my_d], dst_ref=got.at[my_g, sender],
             send_sem=send_d.at[d], recv_sem=recv_d.at[sender],
             device_id=(my_g, d), device_id_type=pl.DeviceIdType.MESH)
 
-    for k in range(1, groups):
-        group_copy(k, my_g).start()
+    for k in range(1, members):
+        member_copy(k, my_d).start()
 
     def spread(c, carry):
         at = pl.ds(pl.multiple_of(c * LANE, LANE), LANE)
@@ -125,20 +133,20 @@
             wide[f, at, :] = jnp.broadcast_to(cols[:, f:f + 1], (LANE, LANE))
         return carry
 
-    first = chunks // 4
+    first = chunks // 2
     lax.fori_loop(0, first, spread, 0)
+    for k in range(1, members):
+        member_copy(k, lax.rem(my_d + k, members)).wait_recv()
+    for k in range(1, groups):
+        group_copy(k, my_g).start()
+    lax.fori_loop(first, chunks, spread, 0)
     for k in range(1, groups):
         group_copy(k, lax.rem(my_g + k, groups)).wait_recv()
-    for k in range(1, members):
-        member_copy(k, my_d).start()
-    lax.fori_loop(first, chunks, spread, 0)
-    for k in range(1, members):
-        member_copy(k, lax.rem(my_d + k, members)).wait_recv()
 
     same = [jnp.zeros((SUB, LANE), jnp.float32)] * 3
     swap = [jnp.zeros((SUB, LANE), jnp.float32)] * 3
     for d in range(ndev):
-        rows = got[d % members, d // members]
+        rows = got[d // members, d % members]
         turned = pltpu.roll(rows, HALF, 1)
         from_d = idx >= d * count
         for i in range(3):
@@ -230,22 +238,23 @@
     both = pl.pallas_call(
         functools.partial(kernel, groups, members),
         out_shape=jax.ShapeDtypeStruct((2, 3, per), jnp.float32),
-        in_specs=[pl.BlockSpec(memory_space=pl.ANY)] * 4,
+        in_specs=[pl.BlockSpec(memory_space=pltpu.HBM)] * 4,
         out_specs=pl.BlockSpec(memory_space=pltpu.VMEM),
         scratch_shapes=[
             pltpu.VMEM((SUB, LANE), jnp.int32),
             pltpu.VMEM((2, 3, count), jnp.float32),
             pltpu.VMEM((count // LANE, LANE), jnp.float32),
             pltpu.VMEM((7, count, LANE), jnp.float32),
-            pltpu.VMEM((members, groups, 3, LANE), jnp.float32),
+            pltpu.VMEM((groups, members, 3, LANE), jnp.float32),
             pltpu.VMEM((ndev // ngrp, ngrp, nrow, LANE), jnp.float32),
             pltpu.VMEM((ndev, nrow, LANE), jnp.float32),
             sems((4,)), sems((groups,)), sems((groups,)), sems((members,)), sems((members,)),
             sems((ndev,)), sems((ndev,)),
         ],
-        compiler_params=pltpu.CompilerParams(collective_id=0, has_side_effects=True),
+        compiler_params=pltpu.CompilerParams(collective_id=0, has_side_effects=True, vmem_limit_bytes=16 << 20),
         name="hermite",
-    )(active_index.reshape(SUB, LANE), positions, velocities, masses.reshape(count // LANE, LANE))
+    )(*[pltpu.with_memory_space_constraint(x, pltpu.HBM) for x in (
+        active_index.reshape(SUB, LANE), positions, velocities, masses.reshape(count // LANE, LANE))])
     return both[0], both[1]
 
 

time: 27.3 us -> 25.3 us (0.927)
  Pallas kernels: 25.2 us -> 23.9 us
  local copies, waits for them, and re-layouts: 1.26 us -> 0.59 us
    pallas_call x1, Pallas kernels: 25.2 us -> 23.9 us  [fused(): pl.pallas_call(functools.partial(kernel, groups, members), out_shape=jax....]
    squeeze x1, local copies, waits for them, and re-layouts: 1.26 us -> 0.59 us  [fused(): return (both[0], both[1])]
where the time goes in v3:
time: 25.3 us; the launch traced here: 25.2 us
  Pallas kernels  23.9 us (94%)
  between operations  0.64 us (3%)
  local copies, waits for them, and re-layouts  0.59 us (2%)
    pallas_call x1, Pallas kernels, fused(): pl.pallas_call(functools.partial(kernel, groups, members), out_shape=jax....  23.9 us
    squeeze x1, local copies, waits for them, and re-layouts, fused(): return (both[0], both[1])  0.59 us

profile of v3, /device:TPU:0, one launch (start us, length us, event | category | flops | bytes accessed | tf_op | source)
XLA Modules:
  0.0 25.2 jit_solution(2550606112578946878)
XLA Ops:
  0.6 23.9 %hermite.1 = f32[2,3,32]{2,1,0:T(4,128)S(1)} custom-call(s32[8,128]{1,0:T(8,128)} %bitcast.6, f32[3,1024]{1,0:T(4,128)} %pos_h.1, f32[3,1024]{1,0:T(4,128)} %vel_h.1, f32[8,128]{1,0:T(8,128)} %bitcast.7), custom_call_target="tpu_custom_call" | custom-call | tf_op jit(solution)/shard_map/hermite/pallas_call | solution.py:238
  24.6 0.6 %slice_bitcast_fusion = (f32[3,32]{1,0:T(4,128)}, f32[3,32]{1,0:T(4,128)}) fusion(f32[2,3,32]{2,1,0:T(4,128)S(1)} %hermite.1), kind=kLoop, calls=%fused_computation | loop fusion | bytes 1536 | tf_op jit(solution)/shard_map/squeeze | solution.py:258

commit v4 on v3

--- a/solution.py
+++ b/solution.py
@@ -202,10 +202,6 @@
             device_id=(lax.div(other, members), lax.rem(other, members)),
             device_id_type=pl.DeviceIdType.MESH)
 
-    def start_b(k, c):
-        scatter_copy(k, me).start()
-        return c
-
     def wait_b(k, c):
         scatter_copy(k, lax.rem(me + k, ndev)).wait_recv()
         return c
@@ -214,7 +210,17 @@
         scatter_copy(k, me).wait_send()
         return c
 
-    lax.fori_loop(1, ndev, start_b, 0)
+    places = [lax.rem(my_d + k, members) for k in range(members)]
+    places = [(d, lax.div(d, ngrp), lax.rem(d, ngrp)) for d in places]
+    for j in reversed(range(groups)):
+        g = lax.rem(my_g + j, groups)
+        for k in sorted(range(members), key=lambda k: abs(2 * k - members)):
+            if j or k:
+                d, block, turn = places[k]
+                pltpu.make_async_remote_copy(
+                    src_ref=part.at[g * (members // ngrp) + block, turn], dst_ref=parts.at[me],
+                    send_sem=send_b.at[g * members + d], recv_sem=recv_b.at[me],
+                    device_id=(g, d), device_id_type=pl.DeviceIdType.MESH).start()
     parts[me] = part[lax.div(me, ngrp), lax.rem(me, ngrp)]
     for k in range(1, groups):
         group_copy(k, my_g).wait_send()
@@ -265,7 +271,7 @@
     def body(positions, velocities, masses, active_index):
         active, count = active_index.shape[0], positions.shape[1]
         per = active // ndev
-        fits = active == SUB * LANE and LANE % per == 0 and ndev == SUB * (LANE // per)
+        fits = active == SUB * LANE and LANE % per == 0 and members % (LANE // per) == 0 and ndev == SUB * (LANE // per)
         if fits and 2 * per == HALF and count % (SUB * LANE) == 0:
             return fused(groups, members, positions, velocities, masses, active_index)
         return per_device(positions, velocities, masses, active_index)

time: 25.3 us -> 25.3 us (level)
  no operation moved by 1% of the time
where the time goes in v4:
time: 25.3 us; the launch traced here: 25.1 us
  Pallas kernels  23.9 us (94%)
  between operations  0.64 us (3%)
  local copies, waits for them, and re-layouts  0.59 us (2%)
    pallas_call x1, Pallas kernels, fused(): pl.pallas_call(functools.partial(kernel, groups, members), out_shape=jax....  23.9 us
    squeeze x1, local copies, waits for them, and re-layouts, fused(): return (both[0], both[1])  0.59 us

profile of v4, /device:TPU:0, one launch (start us, length us, event | category | flops | bytes accessed | tf_op | source)
XLA Modules:
  0.0 25.1 jit_solution(13540759471420667104)
XLA Ops:
  0.6 23.9 %hermite.1 = f32[2,3,32]{2,1,0:T(4,128)S(1)} custom-call(s32[8,128]{1,0:T(8,128)} %bitcast.6, f32[3,1024]{1,0:T(4,128)} %pos_h.1, f32[3,1024]{1,0:T(4,128)} %vel_h.1, f32[8,128]{1,0:T(8,128)} %bitcast.7), custom_call_target="tpu_custom_call" | custom-call | tf_op jit(solution)/shard_map/hermite/pallas_call | solution.py:244
  24.5 0.6 %slice_bitcast_fusion = (f32[3,32]{1,0:T(4,128)}, f32[3,32]{1,0:T(4,128)}) fusion(f32[2,3,32]{2,1,0:T(4,128)S(1)} %hermite.1), kind=kLoop, calls=%fused_computation | loop fusion | bytes 1536 | tf_op jit(solution)/shard_map/squeeze | solution.py:264
